TPU v7x, 32 devices: a whole 2x2x4 slice. The times are simulated.
32 devices in a mesh: dp: 8 (over y, x, core), rep: 4 (over z).
Axes of the slice: x: 2, y: 2, z: 4, core: 2. Of those that a mesh axis runs over, the one named last changes fastest.
Arguments:
- student_in: bfloat16 [16384, 320], P(('dp', 'rep')), may hold values from -6 to 6
- target_in: bfloat16 [16384, 320], P(('dp', 'rep')), may hold values from -6 to 6
- timesteps: int32 [64], P(('dp', 'rep')), may hold values from 20 to 999
- student_win: float32 [1280, 320], P('dp'), may hold values from -0.3125 to 0.3125
- student_wout: float32 [640, 320], P('dp'), may hold values from -0.25 to 0.25
- student_wtime: float32 [640, 320], P('dp'), may hold values from -0.25 to 0.25
- student_gain: float32 [320], replicated, may hold values from 0.5 to 1.5
- student_bias: float32 [320], replicated, may hold values from -3 to 3
- target_win: float32 [1280, 320], P('dp'), may hold values from -0.3125 to 0.3125
- target_wout: float32 [640, 320], P('dp'), may hold values from -0.25 to 0.25
- target_wtime: float32 [640, 320], P('dp'), may hold values from -0.25 to 0.25
- target_gain: float32 [320], replicated, may hold values from 0.5 to 1.5
- target_bias: float32 [320], replicated, may hold values from -3 to 3
Outputs:
- grad_win: float32 [1280, 320], P('dp')
- grad_wout: float32 [640, 320], P('dp')
- grad_wtime: float32 [640, 320], P('dp')
- grad_gain: float32 [320], replicated
- grad_bias: float32 [320], replicated
- ema_win: float32 [1280, 320], P('dp')
- ema_wout: float32 [640, 320], P('dp')
- ema_wtime: float32 [640, 320], P('dp')
- ema_gain: float32 [320], replicated
- ema_bias: float32 [320], replicated
Inputs may be any that keep to these rules, and one draw needn't show every extreme that they name: `timesteps`: student timestep of each sample; the target is evaluated at 20 steps earlier.
All inputs are finite; a program needn't handle non-finite values.
Results may differ from a plain program's by a relative error of at most 0.004.
The roundings to bfloat16 on the way count: a program that leaves them out, or rounds other values in their place, can miss the bound.
Values may be sent and summed in bfloat16 or wider, within the bound.
A program may use at most 64 MiB of HBM per device.

v0:
```python
import math

import jax
import jax.numpy as jnp
from jax import lax
from jax.sharding import PartitionSpec as P

SKIP = 20


ema_decay = 0.95
learn_rate = 0.05


def sinusoid(step_ids, width):
    half_width = width // 2
    frequency = jnp.exp(-math.log(10000.0) * jnp.arange(half_width, dtype=jnp.float32) / half_width)
    angles = step_ids.astype(jnp.float32)[:, None] * frequency[None, :]
    return jnp.concatenate([jnp.cos(angles), jnp.sin(angles)], axis=1)


def gelu_tanh(value):
    inner = 0.7978845608 * (value + 0.044715 * value * value * value)
    return 0.5 * value * (1.0 + jnp.tanh(inner))


def gelu_slope(value):
    tangent = jnp.tanh(0.7978845608 * (value + 0.044715 * value * value * value))
    return 0.5 * (1.0 + tangent) + 0.5 * value * (1.0 - tangent * tangent) * 0.7978845608 * (
        1.0 + 0.134145 * value * value
    )


def contract_last(left, right):
    return lax.dot_general(
        left, right, (((1,), (1,)), ((), ())), preferred_element_type=jnp.float32
    )


def contract_first(left, right):
    return lax.dot_general(
        left, right, (((0,), (0,)), ((), ())), preferred_element_type=jnp.float32
    )


def forward(tok_rows, step_ids, w_in, w_out, w_time, gain, bias):
    time_feat = jax.nn.silu(sinusoid(step_ids, w_time.shape[0])).astype(jnp.bfloat16)
    embedding = jnp.dot(time_feat, w_time, preferred_element_type=jnp.float32)
    samples = step_ids.shape[0]
    width = tok_rows.shape[1]
    summed = tok_rows.astype(jnp.float32).reshape(samples, -1, width) + embedding[:, None, :]
    summed = summed.reshape(-1, width)
    center = summed - jnp.mean(summed, axis=1, keepdims=True)
    inv_std = lax.rsqrt(jnp.mean(center * center, axis=1, keepdims=True) + 1e-05)
    normed = center * inv_std
    normed_b = (normed * gain + bias).astype(jnp.bfloat16)
    mixed = contract_last(normed_b, w_in)
    hidden_count = w_out.shape[0]
    gate_part = mixed[:, :hidden_count]
    up_part = mixed[:, hidden_count:]
    gelu_gate = gelu_tanh(gate_part)
    hidden = (gelu_gate * up_part).astype(jnp.bfloat16)
    output = summed + jnp.dot(hidden, w_out, preferred_element_type=jnp.float32)
    return (output, (time_feat, normed, inv_std, normed_b, gate_part, up_part, gelu_gate, hidden))


def backward(grad_y, saved, w_in, w_out, gain):
    time_feat, normed, inv_std, normed_b, gate_part, up_part, gelu_gate, hidden = saved
    grad_yb = grad_y.astype(jnp.bfloat16)
    grad_h = contract_last(grad_yb, w_out)
    grad_mix = jnp.concatenate(
        [grad_h * up_part * gelu_slope(gate_part), grad_h * gelu_gate], axis=1
    ).astype(jnp.bfloat16)
    grad_z = jnp.dot(grad_mix, w_in, preferred_element_type=jnp.float32)
    grad_gain = jnp.sum(grad_z * normed, axis=0)
    grad_bias = jnp.sum(grad_z, axis=0)
    grad_n = grad_z * gain
    grad_s = grad_y + inv_std * (
        grad_n
        - jnp.mean(grad_n, axis=1, keepdims=True)
        - normed * jnp.mean(grad_n * normed, axis=1, keepdims=True)
    )
    samples = time_feat.shape[0]
    grad_emb = jnp.sum(grad_s.reshape(samples, -1, grad_s.shape[1]), axis=1)
    grad_time = lax.dot_general(
        time_feat.astype(jnp.float32),
        grad_emb,
        (((0,), (0,)), ((), ())),
        precision=lax.Precision.HIGHEST,
        preferred_element_type=jnp.float32,
    )
    return (grad_yb, grad_mix, grad_gain, grad_bias, grad_time)


def fetch(piece_in, piece_out, piece_time):
    return (
        lax.all_gather(piece_in, "dp", axis=0, tiled=True),
        lax.all_gather(piece_out, "dp", axis=0, tiled=True),
        lax.all_gather(piece_time, "dp", axis=0, tiled=True),
    )


def per_device(
    student_in,
    target_in,
    timesteps,
    student_win,
    student_wout,
    student_wtime,
    student_gain,
    student_bias,
    target_win,
    target_wout,
    target_wtime,
    target_gain,
    target_bias,
):
    s_in, s_out, s_time = fetch(
        student_win.astype(jnp.bfloat16),
        student_wout.astype(jnp.bfloat16),
        student_wtime.astype(jnp.bfloat16),
    )
    student_out, saved = forward(
        student_in, timesteps, s_in, s_out, s_time, student_gain, student_bias
    )
    t_in, t_out, t_time = fetch(
        target_win.astype(jnp.bfloat16),
        target_wout.astype(jnp.bfloat16),
        target_wtime.astype(jnp.bfloat16),
    )
    target_out, unused = forward(
        target_in, timesteps - SKIP, t_in, t_out, t_time, target_gain, target_bias
    )
    grad_y = (student_out - target_out) / student_in.shape[0]
    back_in, back_out = (
        lax.all_gather(student_win.astype(jnp.bfloat16), "dp", axis=0, tiled=True),
        lax.all_gather(student_wout.astype(jnp.bfloat16), "dp", axis=0, tiled=True),
    )
    grad_yb, grad_mix, grad_gain, grad_bias, grad_time = backward(
        grad_y, saved, back_in, back_out, student_gain
    )
    normed_b = saved[3]
    hidden = saved[7]
    part = grad_mix
    shard_in = lax.psum_scatter(
        contract_first(part, normed_b), "dp", scatter_dimension=0, tiled=True
    )
    part = hidden
    shard_out = lax.psum_scatter(
        contract_first(part, grad_yb), "dp", scatter_dimension=0, tiled=True
    )
    shard_time = lax.psum_scatter(grad_time, "dp", scatter_dimension=0, tiled=True)
    shard_in, shard_out, shard_time = lax.psum((shard_in, shard_out, shard_time), "rep")
    total_gain, total_bias = lax.psum((grad_gain, grad_bias), ("dp", "rep"))

    def average(target_p, student_p, grad_p):
        return ema_decay * target_p + (1.0 - ema_decay) * (student_p - learn_rate * grad_p)

    return (
        shard_in,
        shard_out,
        shard_time,
        total_gain,
        total_bias,
        average(target_win, student_win, shard_in),
        average(target_wout, student_wout, shard_out),
        average(target_wtime, student_wtime, shard_time),
        average(target_gain, student_gain, total_gain),
        average(target_bias, student_bias, total_bias),
    )


def solution(mesh):
    in_specs = (
        P(("dp", "rep"), None),
        P(("dp", "rep"), None),
        P(("dp", "rep")),
        P("dp", None),
        P("dp", None),
        P("dp", None),
        P(),
        P(),
        P("dp", None),
        P("dp", None),
        P("dp", None),
        P(),
        P(),
    )
    out_specs = (
        P("dp", None),
        P("dp", None),
        P("dp", None),
        P(),
        P(),
        P("dp", None),
        P("dp", None),
        P("dp", None),
        P(),
        P(),
    )
    return jax.shard_map(
        per_device, mesh=mesh, in_specs=in_specs, out_specs=out_specs, check_vma=False
    )
```

profile of v0, /device:TPU:0, one launch (start us, length us, event | category | flops | bytes accessed | tf_op | source)
XLA Modules:
  0.0 256.5 jit_solution(1124549243400351824)
XLA Ops:
  7.2 0.7 fusion.50
  8.0 0.9 convert_element_type.62
  8.9 0.9 convert_element_type.58
  9.8 0.9 convert_element_type.70
  10.7 0.9 convert_element_type.66
  11.6 1.0 convert_element_type.60
  12.6 1.0 convert_element_type.68
  13.6 11.3 %all_gather.22 = bf16[640,320]{1,0:T(8,128)(2,1)S(1)} all-gather(bf16[80,320]{1,0:T(8,128)(2,1)S(1)} %convert_element_type.62), channel_id=1, replica_groups=mesh['dp'=8,'rep'=4] {'dp'}, dimensions={0}, use_global_device_ids=true | all-gather | bytes 460800 | tf_op jit(solution)/shard_map/all_gather | solution.py:98
  24.9 9.8 %all_gather.23 = bf16[640,320]{1,0:T(8,128)(2,1)S(1)} all-gather(bf16[80,320]{1,0:T(8,128)(2,1)S(1)} %convert_element_type.66), channel_id=1, replica_groups=mesh['dp'=8,'rep'=4] {'dp'}, dimensions={0}, use_global_device_ids=true | all-gather | bytes 460800 | tf_op jit(solution)/shard_map/all_gather | solution.py:99
  34.7 8.9 %all_gather.25 = bf16[640,320]{1,0:T(8,128)(2,1)S(1)} all-gather(bf16[80,320]{1,0:T(8,128)(2,1)S(1)} %convert_element_type.70), channel_id=1, replica_groups=mesh['dp'=8,'rep'=4] {'dp'}, dimensions={0}, use_global_device_ids=true | all-gather | bytes 460800 | tf_op jit(solution)/shard_map/all_gather | solution.py:98
  43.6 9.8 %all_gather.20 = bf16[640,320]{1,0:T(8,128)(2,1)S(1)} all-gather(bf16[80,320]{1,0:T(8,128)(2,1)S(1)} %convert_element_type.58), channel_id=1, replica_groups=mesh['dp'=8,'rep'=4] {'dp'}, dimensions={0}, use_global_device_ids=true | all-gather | bytes 460800 | tf_op jit(solution)/shard_map/all_gather | solution.py:99
  53.4 0.2 multiply_cosine_fusion.1
  53.6 0.3 fusion.46
  53.9 0.4 add.123
  54.8 0.3 fusion.33
  55.2 0.4 add.133
  55.6 0.2 copy-done.4
  56.1 10.0 %all_gather.21 = bf16[1280,320]{1,0:T(8,128)(2,1)S(1)} all-gather(bf16[160,320]{1,0:T(8,128)(2,1)S(1)} %convert_element_type.60), channel_id=1, replica_groups=mesh['dp'=8,'rep'=4] {'dp'}, dimensions={0}, use_global_device_ids=true | all-gather | bytes 921600 | tf_op jit(solution)/shard_map/all_gather | solution.py:97
  66.1 10.9 %all_gather.24 = bf16[1280,320]{1,0:T(8,128)(2,1)S(1)} all-gather(bf16[160,320]{1,0:T(8,128)(2,1)S(1)} %convert_element_type.68), channel_id=1, replica_groups=mesh['dp'=8,'rep'=4] {'dp'}, dimensions={0}, use_global_device_ids=true | all-gather | bytes 921600 | tf_op jit(solution)/shard_map/all_gather | solution.py:97
  77.0 1.0 fusion.48
  78.1 0.5 multiply_convert_fusion.1
  78.5 0.2 copy-done.18
  78.7 1.0 fusion.21
  79.8 0.7 convolution_add_fusion
  80.5 0.5 fusion.14
  81.0 0.8 copy-done
  81.9 1.5 fusion.26
  83.4 0.2 reduce-scatter.8.cloned.1.call-start
  83.6 2.6 %fusion.12 = (bf16[512,640]{1,0:T(8,128)(2,1)S(1)}, bf16[512,640]{1,0:T(8,128)(2,1)S(1)}) fusion(f32[512,1280]{1,0:T(8,128)S(1)} %fusion.48, bf16[640,320]{1,0:T(8,128)(2,1)} %copy-done.5, f32[512,320]{0,1:T(8,128)} %copy-done), kind=kOutput, calls=%fused_computation.15 | convolution fusion | flops 217415680 | bytes 4997120 | tf_op jit(solution)/shard_map/dot_general | solution.py:35
  86.3 0.9 multiply_reduce_fusion
  87.3 0.5 copy-done.1
  87.8 0.2 multiply_add_fusion.2
  88.1 0.4 reshape.74
  88.5 0.4 reduce_sum.87
  88.9 1.6 fusion.44
  90.7 2.2 fusion.16
  93.0 26.5 %reduce-scatter.6.cloned.1.call-done = f32[80,320]{1,0:T(8,128)} async-done(((f32[640,320]{1,0:T(8,128)}), f32[80,320]{1,0:T(8,128)}) %reduce-scatter.6.cloned.1.call-update) | async-done | bytes 102416 | tf_op jit(solution)/shard_map/reduce_scatter | solution.py:149
  119.5 39.0 %reduce-scatter.8.cloned.1.call-done = f32[80,320]{1,0:T(8,128)} async-done(((f32[640,320]{1,0:T(8,128)}), f32[80,320]{1,0:T(8,128)}) %reduce-scatter.8.cloned.1.call-update) | async-done | bytes 102416 | tf_op jit(solution)/shard_map/reduce_scatter | solution.py:152
  158.5 43.6 %reduce-scatter.4.cloned.1.call-done = f32[160,320]{1,0:T(8,128)} async-done(((f32[1280,320]{1,0:T(8,128)}), f32[160,320]{1,0:T(8,128)}) %reduce-scatter.4.cloned.1.call-update) | async-done | bytes 204816 | tf_op jit(solution)/shard_map/reduce_scatter | solution.py:145
  202.1 39.6 %all-reduce = (f32[320]{0:T(512)S(1)}, f32[320]{0:T(512)S(1)}) all-reduce(f32[320]{0:T(512)S(1)} %get-tuple-element.10, f32[320]{0:T(512)S(1)} %get-tuple-element.13), channel_id=1, replica_groups=mesh['dp'=8,'rep'=4] {'dp','rep'}, use_global_device_ids=true, to_apply=%region_14.15 | all-reduce | flops 640 | bytes 5120 | tf_op jit(solution)/shard_map/psum | solution.py:154
  241.7 0.6 multiply_add_fusion.6
  242.3 0.7 all-reduce.4.cloned.1.call-done
  243.0 1.6 multiply_add_fusion.5
  244.6 1.6 multiply_add_fusion.4
  246.2 1.7 multiply_add_fusion.3
  247.9 0.7 copy.34
  248.6 0.6 copy.35
  249.3 0.6 copy.36
  (67 shorter events, 1.2 us)
Async XLA Ops:
  7.2 112.4 %reduce-scatter.6.cloned.1.call-start = ((), (), s32[]{:S(2)}) async-start(), calls=%async_computation.4 | async-start | bytes 1105920 | tf_op jit(solution)/shard_map/reduce_scatter | solution.py:149
  24.9 55.6 %copy-start.5 = (bf16[640,320]{1,0:T(8,128)(2,1)}, bf16[640,320]{1,0:T(8,128)(2,1)S(1)}, u32[]{:S(2)}) copy-start(bf16[640,320]{1,0:T(8,128)(2,1)S(1)} %all_gather.22) | copy-start | bytes 1228804
  53.5 1.0 copy-start.15
  54.8 1.0 copy-start.4
  56.1 21.0 %copy-start.16 = (f32[320]{0:T(512)S(1)}, f32[320]{0:T(512)}, u32[]{:S(2)}) copy-start(f32[320]{0:T(512)} %param.19) | copy-start | bytes 3844
  56.1 21.0 %copy-start.17 = (f32[320]{0:T(512)S(1)}, f32[320]{0:T(512)}, u32[]{:S(2)}) copy-start(f32[320]{0:T(512)} %param.20) | copy-start | bytes 3844
  66.1 10.9 %copy-start.2 = (bf16[1280,320]{1,0:T(8,128)(2,1)}, bf16[1280,320]{1,0:T(8,128)(2,1)S(1)}, u32[]{:S(2)}) copy-start(bf16[1280,320]{1,0:T(8,128)(2,1)S(1)} %all_gather.21) | copy-start | bytes 2457604
  78.0 0.7 copy-start.18
  78.1 0.7 copy-start.19
  81.0 0.8 copy-start
  83.4 75.1 %reduce-scatter.8.cloned.1.call-start = ((), (), s32[]{:S(2)}) async-start(), calls=%async_computation.5 | async-start | bytes 1105920 | tf_op jit(solution)/shard_map/reduce_scatter | solution.py:152
  83.6 2.7 %copy-start.3 = (bf16[1280,320]{1,0:T(8,128)(2,1)S(1)}, bf16[1280,320]{1,0:T(8,128)(2,1)}, u32[]{:S(2)}) copy-start(bf16[1280,320]{1,0:T(8,128)(2,1)} %copy-done.2) | copy-start | bytes 2457604
  86.3 0.9 copy-start.22
  86.3 1.0 copy-start.24
  86.3 1.6 copy-start.1
  88.5 2.1 copy-start.23
  88.9 1.7 copy-start.25
  90.6 111.5 %reduce-scatter.4.cloned.1.call-start = ((), (), s32[]{:S(2)}) async-start(), calls=%async_computation.3 | async-start | bytes 2211840 | tf_op jit(solution)/shard_map/reduce_scatter | solution.py:145
  92.9 150.1 %copy-start.9 = (f32[80,320]{1,0:T(8,128)S(1)}, f32[80,320]{1,0:T(8,128)}, u32[]{:S(2)}) copy-start(f32[80,320]{1,0:T(8,128)} %param.22) | copy-start | bytes 307204
  92.9 150.1 %copy-start.10 = (f32[80,320]{1,0:T(8,128)S(1)}, f32[80,320]{1,0:T(8,128)}, u32[]{:S(2)}) copy-start(f32[80,320]{1,0:T(8,128)} %param.17) | copy-start | bytes 307204
  92.9 151.7 %copy-start.11 = (f32[80,320]{1,0:T(8,128)S(1)}, f32[80,320]{1,0:T(8,128)}, u32[]{:S(2)}) copy-start(f32[80,320]{1,0:T(8,128)} %param.18) | copy-start | bytes 307204
  92.9 151.7 %copy-start.12 = (f32[80,320]{1,0:T(8,128)S(1)}, f32[80,320]{1,0:T(8,128)}, u32[]{:S(2)}) copy-start(f32[80,320]{1,0:T(8,128)} %param.23) | copy-start | bytes 307204
  92.9 153.3 %copy-start.6 = (f32[160,320]{1,0:T(8,128)S(1)}, f32[160,320]{1,0:T(8,128)}, u32[]{:S(2)}) copy-start(f32[160,320]{1,0:T(8,128)} %param.16) | copy-start | bytes 614404
  92.9 153.3 %copy-start.7 = (f32[160,320]{1,0:T(8,128)S(1)}, f32[160,320]{1,0:T(8,128)}, u32[]{:S(2)}) copy-start(f32[160,320]{1,0:T(8,128)} %param.21) | copy-start | bytes 614404
  93.0 150.0 %all-reduce.4.cloned.1.call-start = ((), (), s32[]{:S(2)}) async-start(), calls=%async_computation.6 | async-start | bytes 983040 | tf_op jit(solution)/shard_map/psum | solution.py:153
  241.7 7.6 %copy-start.20 = (f32[320]{0:T(512)}, f32[320]{0:T(512)S(1)}, u32[]{:S(2)}) copy-start(f32[320]{0:T(512)S(1)} %get-tuple-element.39) | copy-start | bytes 3844
  241.7 7.6 %copy-start.21 = (f32[320]{0:T(512)}, f32[320]{0:T(512)S(1)}, u32[]{:S(2)}) copy-start(f32[320]{0:T(512)S(1)} %get-tuple-element.40) | copy-start | bytes 3844
  243.0 4.9 %copy-start.8 = (f32[160,320]{1,0:T(8,128)S(1)}, f32[160,320]{1,0:T(8,128)}, u32[]{:S(2)}) copy-start(f32[160,320]{1,0:T(8,128)} %get-tuple-element.36) | copy-start | bytes 614404
  243.0 5.6 %copy-start.14 = (f32[80,320]{1,0:T(8,128)S(1)}, f32[80,320]{1,0:T(8,128)}, u32[]{:S(2)}) copy-start(f32[80,320]{1,0:T(8,128)} %get-tuple-element.37) | copy-start | bytes 307204
  243.0 6.3 %copy-start.13 = (f32[80,320]{1,0:T(8,128)S(1)}, f32[80,320]{1,0:T(8,128)}, u32[]{:S(2)}) copy-start(f32[80,320]{1,0:T(8,128)} %get-tuple-element.38) | copy-start | bytes 307204
Sparse Core Ops, SparseCore 0:
  83.5 35.9 reduce-scatter.5
  122.8 35.7 reduce-scatter.7
  161.9 40.1 reduce-scatter.3
  204.5 38.4 all-reduce.3
where the time goes:
time: 257 us; the launch traced here: 256 us
  waiting for transfers between devices  110 us (43%)
  blocking collectives  100 us (39%)
  between operations  14.1 us (5%)
  other arithmetic  13.6 us (5%)
  matrix products  12.8 us (5%)
  local copies, waits for them, and re-layouts  5.4 us (2%)
    reduce_scatter x1, waiting for transfers between devices, per_device(): lax.psum_scatter(contract_first(part, normed_b), 'dp', scatter_dimension=...  43.6 us
    psum x1, blocking collectives, per_device(): total_gain, total_bias = lax.psum((grad_gain, grad_bias), ('dp', 'rep'))  39.6 us
    reduce_scatter x1, waiting for transfers between devices, per_device(): lax.psum_scatter(grad_time, 'dp', scatter_dimension=0, tiled=True)  39 us
    reduce_scatter x1, waiting for transfers between devices, per_device(): lax.psum_scatter(contract_first(part, grad_yb), 'dp', scatter_dimension=0...  26.5 us
    all_gather x2, blocking collectives, fetch(): lax.all_gather(piece_in, 'dp', axis=0, tiled=True)  20.9 us
    all_gather x2, blocking collectives, fetch(): lax.all_gather(piece_out, 'dp', axis=0, tiled=True)  20.2 us
    all_gather x2, blocking collectives, fetch(): lax.all_gather(piece_time, 'dp', axis=0, tiled=True)  19.6 us
    add x4, other arithmetic, average(): ema_decay * target_p + (1.0 - ema_decay) * (student_p - learn_rate * grad_p)  5.5 us
  transfers between devices with their start and end apart: 4, of which 4 were waited for; matrix products, arithmetic and copies ran while one was open for 4% of the time, Pallas kernels for 0%

commit v1 on v0

--- a/solution.py
+++ b/solution.py
@@ -1,9 +1,15 @@
+import functools
 import math
 
 import jax
 import jax.numpy as jnp
 from jax import lax
+from jax.experimental import pallas as pl
+from jax.experimental.pallas import tpu as pltpu
 from jax.sharding import PartitionSpec as P
+
+MESH = pl.DeviceIdType.MESH
+SUB = 8
 
 SKIP = 20
 
@@ -170,6 +176,375 @@
     )
 
 
+def time_features(step_ids, width):
+    return jax.nn.silu(sinusoid(step_ids, width)).astype(jnp.bfloat16)
+
+
+def fused_kernel(
+    n_rep, n_sam,
+    x_s, x_t, tf, sw, so, st, sg, sb, tw, to, tt, tg, tb,
+    gw_o, go_o, gt_o, gg_o, gb_o, ew_o, eo_o, et_o, eg_o, eb_o,
+    ws_all, os_all, wt_all, ot_all,
+    tf_all, e_part, e_in, small, small_rep,
+    normed_v, inv_v, nb_v, hid_v, a_v, b_v, y_v, nbt_v, gyb_v, gma_v, gmb_v,
+    g_win, g_out, gb_win, gb_out, r1_win, r1_out, s2_win, s2_out, r2_win, r2_out,
+    p_v, pb_v, r3_v, fin_v,
+    g_send, g_recv, tf_send, tf_recv, e_send, e_recv, sm_send, sm_recv,
+    r1_send, r1_recv, r2_send, r2_recv, r3_send, r3_recv, r4_send, r4_recv, rs_send, rs_recv,
+):
+    f32, bf16 = jnp.float32, jnp.bfloat16
+    me, rep = lax.axis_index("dp"), lax.axis_index("rep")
+    core, col, row = lax.rem(me, 2), lax.rem(lax.div(me, 2), 2), lax.div(me, 4)
+    rows_in, rows_out, rows_time = sw.shape[0], so.shape[0], st.shape[0]
+    tokens = x_s.shape[0]
+    per = tokens // n_sam
+    ff = os_all.shape[0]
+
+    def peer(t):
+        flip = lambda b, on: 1 - b if on else b
+        return flip(row, t & 4) * 4 + flip(col, t & 2) * 2 + flip(core, t & 1)
+
+    def dp_id(t):
+        return {"dp": peer(t)}
+
+    def rep_at(j):
+        return lax.rem(rep + j, n_rep)
+
+    sends = []
+
+    def send(src, dst, s_sem, r_sem, where):
+        copy = pltpu.make_async_remote_copy(
+            src_ref=src, dst_ref=dst, send_sem=s_sem, recv_sem=r_sem,
+            device_id=where, device_id_type=MESH,
+        )
+        copy.start()
+        sends.append(copy)
+
+    def arrive(dst, s_sem, r_sem):
+        pltpu.make_async_remote_copy(
+            src_ref=dst, dst_ref=dst, send_sem=s_sem, recv_sem=r_sem,
+            device_id=dp_id(1), device_id_type=MESH,
+        ).wait_recv()
+
+    def block(ref, owner, count):
+        return ref.at[pl.ds(pl.multiple_of(owner * count, 16), count)]
+
+    bufs = (ws_all, os_all, wt_all, ot_all)
+    counts = (rows_in, rows_out, rows_in, rows_out)
+    firsts = (2, 4, 4, 2)
+    for buf, own, count in zip(bufs, (sw, so, tw, to), counts):
+        buf[pl.ds(pl.multiple_of(me * count, 16), count), :] = own[...].astype(bf16)
+    tf_all[pl.ds(me, 1)] = tf[pl.ds(me, 1)]
+
+    barrier = pltpu.get_barrier_semaphore()
+    for t in range(1, 8):
+        pl.semaphore_signal(barrier, inc=1, device_id=dp_id(t), device_id_type=MESH)
+    for j in range(1, n_rep):
+        pl.semaphore_signal(barrier, inc=1, device_id={"rep": rep_at(j)}, device_id_type=MESH)
+    pl.semaphore_wait(barrier, 7 + n_rep - 1)
+
+    def push(seg, orel, t, k):
+        part = block(bufs[seg], peer(orel), counts[seg])
+        send(part, part, g_send.at[seg * 8 + k], g_recv.at[seg * 8 + (orel ^ t)], dp_id(t))
+
+    def landed(seg, orel):
+        arrive(block(bufs[seg], peer(orel), counts[seg]), g_send.at[0], g_recv.at[seg * 8 + orel])
+
+    def open_gather(seg):
+        push(seg, 0, firsts[seg], 0)
+        push(seg, 0, 6 - firsts[seg], 1)
+        push(seg, 0, 1, 2)
+
+    def relay_near(seg):
+        first, second = firsts[seg], 6 - firsts[seg]
+        landed(seg, first)
+        push(seg, first, second, 3)
+        push(seg, first, 1, 4)
+        landed(seg, second)
+        push(seg, second, 1, 5)
+
+    def relay_far(seg):
+        landed(seg, 6)
+        push(seg, 6, 1, 6)
+
+    def close_gather(seg):
+        for orel in (1, 3, 5, 7):
+            landed(seg, orel)
+
+    for t in range(1, 8):
+        send(tf.at[peer(t)], tf_all.at[me], tf_send.at[t], tf_recv.at[t], dp_id(t))
+    open_gather(0)
+    for t in range(1, 8):
+        arrive(tf_all.at[peer(t)], tf_send.at[t], tf_recv.at[t])
+    feats = tf_all[...].reshape(8 * SUB, rows_time).astype(bf16)
+    part_s = jnp.dot(feats, st[...].astype(bf16), preferred_element_type=f32)
+    part_t = jnp.dot(feats, tt[...].astype(bf16), preferred_element_type=f32)
+    line = lax.rem(lax.broadcasted_iota(jnp.int32, part_s.shape, 0), SUB)
+    e_part[...] = jnp.where(line < n_sam, part_s, part_t).reshape(e_part.shape)
+    e_in[pl.ds(me, 1)] = e_part[pl.ds(me, 1)]
+    for t in range(1, 8):
+        send(e_part.at[peer(t)], e_in.at[me], e_send.at[t], e_recv.at[t], dp_id(t))
+    open_gather(1)
+    open_gather(2)
+    open_gather(3)
+    relay_near(0)
+    for t in range(1, 8):
+        arrive(e_in.at[peer(t)], e_send.at[t], e_recv.at[t])
+    emb = e_in[0]
+    for k in range(1, 8):
+        emb = emb + e_in[k]
+
+    def normalise(x_ref, k, shift, gain, bias):
+        summed = x_ref[pl.ds(k * per, per), :].astype(f32) + shift
+        center = summed - jnp.mean(summed, axis=1, keepdims=True)
+        inv = lax.rsqrt(jnp.mean(center * center, axis=1, keepdims=True) + 1e-05)
+        normed = center * inv
+        return summed, inv, normed, (normed * gain + bias).astype(bf16)
+
+    for k in range(n_sam):
+        at = pl.ds(k * per, per)
+        summed, inv, normed, nb = normalise(x_s, k, emb[k : k + 1], sg[...], sb[...])
+        y_v[at, :], normed_v[at, :], nb_v[at, :] = summed, normed, nb
+        inv_v[at, :] = inv
+    relay_far(0)
+    relay_near(1)
+    for k in range(n_sam):
+        at = pl.ds(k * per, per)
+        summed, inv, normed, nb = normalise(x_t, k, emb[n_sam + k : n_sam + k + 1], tg[...], tb[...])
+        y_v[at, :], nbt_v[at, :] = y_v[at, :] - summed, nb
+    close_gather(0)
+    relay_far(1)
+
+    for k in range(n_sam):
+        at = pl.ds(k * per, per)
+        gate = contract_last(nb_v[at, :], ws_all[:ff, :])
+        up = contract_last(nb_v[at, :], ws_all[ff:, :])
+        tangent = jnp.tanh(0.7978845608 * (gate + 0.044715 * gate * gate * gate))
+        half = 0.5 * (1.0 + tangent)
+        act = gate * half
+        slope = half + 0.5 * gate * (1.0 - tangent * tangent) * 0.7978845608 * (
+            1.0 + 0.134145 * gate * gate
+        )
+        a_v[at, :], b_v[at, :] = up * slope, act
+        hid_v[at, :] = (act * up).astype(bf16)
+        if k == 0:
+            relay_near(2)
+            close_gather(1)
+    relay_far(2)
+    relay_near(3)
+    for k in range(n_sam):
+        at = pl.ds(k * per, per)
+        y_v[at, :] = y_v[at, :] + jnp.dot(hid_v[at, :], os_all[...], preferred_element_type=f32)
+    close_gather(2)
+    relay_far(3)
+
+    for k in range(n_sam):
+        at = pl.ds(k * per, per)
+        gate = contract_last(nbt_v[at, :], wt_all[:ff, :])
+        up = contract_last(nbt_v[at, :], wt_all[ff:, :])
+        hid = (gelu_tanh(gate) * up).astype(bf16)
+        if k == 0:
+            close_gather(3)
+        gy = (y_v[at, :] - jnp.dot(hid, ot_all[...], preferred_element_type=f32)) * (1.0 / tokens)
+        y_v[at, :], gyb_v[at, :] = gy, gy.astype(bf16)
+
+    total_out = contract_first(hid_v[...], gyb_v[...])
+    g_out[...], gb_out[...] = total_out, total_out.astype(bf16)
+
+    def to_core(src, dst, count, q, k):
+        send(block(src, 2 * q + 1 - core, count), dst.at[q], r1_send.at[k], r1_recv.at[k], dp_id(1))
+
+    for q in range(4):
+        to_core(gb_out, r1_out, rows_out, q, q)
+
+    grad_gain = jnp.zeros((1, x_s.shape[1]), f32)
+    grad_bias = grad_gain
+    embs = []
+    for k in range(n_sam):
+        at = pl.ds(k * per, per)
+        gh = contract_last(gyb_v[at, :], os_all[...])
+        gma, gmb = (gh * a_v[at, :]).astype(bf16), (gh * b_v[at, :]).astype(bf16)
+        gma_v[at, :], gmb_v[at, :] = gma, gmb
+        gz = jnp.dot(gma, ws_all[:ff, :], preferred_element_type=f32) + jnp.dot(
+            gmb, ws_all[ff:, :], preferred_element_type=f32
+        )
+        normed = normed_v[at, :]
+        grad_gain = grad_gain + jnp.sum(gz * normed, axis=0, keepdims=True)
+        grad_bias = grad_bias + jnp.sum(gz, axis=0, keepdims=True)
+        gn = gz * sg[...]
+        gs = y_v[at, :] + inv_v[at, :] * (
+            gn
+            - jnp.mean(gn, axis=1, keepdims=True)
+            - normed * jnp.mean(gn * normed, axis=1, keepdims=True)
+        )
+        embs.append(jnp.sum(gs, axis=0, keepdims=True))
+    fill = jnp.zeros((SUB - n_sam - 2, x_s.shape[1]), f32)
+    small[pl.ds(me, 1)] = jnp.concatenate(embs + [grad_gain, grad_bias, fill], axis=0)[None]
+
+    for h, gm in enumerate((gma_v, gmb_v)):
+        total = contract_first(gm[...], nb_v[...])
+        at = pl.ds(h * ff, ff)
+        g_win[at, :], gb_win[at, :] = total, total.astype(bf16)
+        for q in (2 * h, 2 * h + 1):
+            to_core(gb_win, r1_win, rows_in, q, 4 + q)
+        if h == 0:
+            for t in range(1, 8):
+                send(small.at[me], small.at[me], sm_send.at[t], sm_recv.at[t], dp_id(t))
+
+    def pair(g, r1, owner_rel, count):
+        owner = peer(owner_rel)
+        own = g[pl.ds(pl.multiple_of(owner * count, 16), count), :]
+        return own + r1[lax.div(owner, 2)].astype(f32)
+
+    for g, r1, s2, r2, count, base in (
+        (g_out, r1_out, s2_out, r2_out, rows_out, 0),
+        (g_win, r1_win, s2_win, r2_win, rows_in, 4),
+    ):
+        for q in range(4):
+            arrive(r1.at[q], r1_send.at[base + q], r1_recv.at[base + q])
+        for k in (3, 1, 2):
+            s2[k] = pair(g, r1, 2 * k, count).astype(bf16)
+            send(s2.at[k], r2.at[k], r2_send.at[base + k], r2_recv.at[base + k], dp_id(2 * k))
+
+    for t in range(1, 8):
+        arrive(small.at[peer(t)], sm_send.at[t], sm_recv.at[t])
+    feats = tf_all[...].reshape(8 * SUB, rows_time)
+    line = lax.rem(lax.broadcasted_iota(jnp.int32, feats.shape, 0), SUB)
+    feats = jnp.where(line < n_sam, feats, 0.0)
+    p_v[pl.ds(rows_in + rows_out, rows_time), :] = lax.dot_general(
+        feats,
+        small[...].reshape(8 * SUB, x_s.shape[1]),
+        (((0,), (0,)), ((), ())),
+        precision=lax.Precision.HIGHEST,
+        preferred_element_type=f32,
+    )
+    sums = small[0]
+    for k in range(1, 8):
+        sums = sums + small[k]
+    small_rep[pl.ds(rep, 1)] = sums[None]
+    for j in range(1, n_rep):
+        send(small_rep.at[rep], small_rep.at[rep], rs_send.at[j], rs_recv.at[j], {"rep": rep_at(j)})
+
+    for g, r1, r2, count, base, start in (
+        (g_out, r1_out, r2_out, rows_out, 0, rows_in),
+        (g_win, r1_win, r2_win, rows_in, 4, 0),
+    ):
+        total = pair(g, r1, 0, count)
+        for k in (1, 2, 3):
+            arrive(r2.at[k], r2_send.at[base + k], r2_recv.at[base + k])
+            total = total + r2[k].astype(f32)
+        p_v[pl.ds(start, count), :] = total
+    pb_v[...] = p_v[...].astype(bf16)
+
+    share = p_v.shape[0] // n_rep
+    for j in range(1, n_rep):
+        send(block(pb_v, rep_at(j), share), r3_v.at[j], r3_send.at[j], r3_recv.at[j], {"rep": rep_at(j)})
+    mine = pl.ds(pl.multiple_of(rep * share, 16), share)
+    total = p_v[mine, :]
+    for j in range(1, n_rep):
+        arrive(r3_v.at[j], r3_send.at[j], r3_recv.at[j])
+        total = total + r3_v[j].astype(f32)
+    fin_v[mine, :] = total
+    for j in range(1, n_rep):
+        part = block(fin_v, rep, share)
+        send(part, part, r4_send.at[j], r4_recv.at[j], {"rep": rep_at(j)})
+
+    for j in range(1, n_rep):
+        arrive(small_rep.at[rep_at(n_rep - j)], rs_send.at[j], rs_recv.at[j])
+    sums = small_rep[0]
+    for j in range(1, n_rep):
+        sums = sums + small_rep[j]
+
+    def average(target_p, student_p, grad_p):
+        return ema_decay * target_p + (1.0 - ema_decay) * (student_p - learn_rate * grad_p)
+
+    gg, gb = sums[n_sam : n_sam + 1], sums[n_sam + 1 : n_sam + 2]
+    gg_o[...], gb_o[...] = gg, gb
+    eg_o[...] = average(tg[...], sg[...], gg)
+    eb_o[...] = average(tb[...], sb[...], gb)
+    for j in range(1, n_rep):
+        arrive(block(fin_v, rep_at(n_rep - j), share), r4_send.at[j], r4_recv.at[j])
+    start = 0
+    for g_o, e_o, student, target in (
+        (gw_o, ew_o, sw, tw), (go_o, eo_o, so, to), (gt_o, et_o, st, tt),
+    ):
+        grad = fin_v[pl.ds(start, g_o.shape[0]), :]
+        g_o[...] = grad
+        e_o[...] = average(target[...], student[...], grad)
+        start += g_o.shape[0]
+    for copy in sends:
+        copy.wait_send()
+
+
+def fused_device(n_dp, n_rep, *args):
+    (student_in, target_in, timesteps, sw, so, st, sg, sb, tw, to, tt, tg, tb) = args
+    f32, bf16 = jnp.float32, jnp.bfloat16
+    tokens, width = student_in.shape
+    n_sam = timesteps.shape[0]
+    rows_in, rows_out, rows_time = sw.shape[0], so.shape[0], st.shape[0]
+    ff = rows_out * n_dp
+    both = jnp.concatenate([timesteps, timesteps - SKIP])
+    feats = time_features(both, rows_time * n_dp).astype(f32)
+    feats = jnp.pad(feats, ((0, SUB - 2 * n_sam), (0, 0)))
+    feats = feats.reshape(SUB, n_dp, rows_time).transpose(1, 0, 2)
+    rows_all = rows_in + rows_out + rows_time
+    vm = pltpu.VMEM
+    dma = pltpu.SemaphoreType.DMA
+    scratch = [
+        vm((n_dp * rows_in, width), bf16), vm((ff, width), bf16),
+        vm((n_dp * rows_in, width), bf16), vm((ff, width), bf16),
+        vm((n_dp, SUB, rows_time), f32), vm((n_dp, SUB, width), f32), vm((n_dp, SUB, width), f32),
+        vm((n_dp, SUB, width), f32), vm((n_rep, SUB, width), f32),
+        vm((tokens, width), f32), vm((tokens, 1), f32), vm((tokens, width), bf16),
+        vm((tokens, ff), bf16), vm((tokens, ff), f32), vm((tokens, ff), f32),
+        vm((tokens, width), f32), vm((tokens, width), bf16), vm((tokens, width), bf16),
+        vm((tokens, ff), bf16), vm((tokens, ff), bf16),
+        vm((n_dp * rows_in, width), f32), vm((ff, width), f32),
+        vm((n_dp * rows_in, width), bf16), vm((ff, width), bf16),
+        vm((4, rows_in, width), bf16), vm((4, rows_out, width), bf16),
+        vm((4, rows_in, width), bf16), vm((4, rows_out, width), bf16),
+        vm((4, rows_in, width), bf16), vm((4, rows_out, width), bf16),
+        vm((rows_all, width), f32), vm((rows_all, width), bf16),
+        vm((n_rep, rows_all // n_rep, width), bf16), vm((rows_all, width), f32),
+        dma((32,)), dma((32,)), dma((8,)), dma((8,)), dma((8,)), dma((8,)), dma((8,)), dma((8,)),
+        dma((8,)), dma((8,)), dma((8,)), dma((8,)),
+        dma((n_rep,)), dma((n_rep,)), dma((n_rep,)), dma((n_rep,)), dma((n_rep,)), dma((n_rep,)),
+    ]
+    line = lambda v: v.reshape(1, width)
+    big = [jax.ShapeDtypeStruct(w.shape, f32) for w in (sw, so, st)]
+    flat = [jax.ShapeDtypeStruct((1, width), f32)] * 2
+    outs = pl.pallas_call(
+        functools.partial(fused_kernel, n_rep, n_sam),
+        out_shape=(*big, *flat, *big, *flat),
+        in_specs=[pl.BlockSpec(memory_space=vm)] * 13,
+        out_specs=[pl.BlockSpec(memory_space=vm)] * 10,
+        scratch_shapes=scratch,
+        compiler_params=pltpu.CompilerParams(
+            collective_id=0, has_side_effects=True, vmem_limit_bytes=60 * 1024 * 1024
+        ),
+        name="distill_step",
+    )(student_in, target_in, feats, sw, so, st, line(sg), line(sb), tw, to, tt, line(tg), line(tb))
+    return tuple(o.reshape(width) if o.shape[0] == 1 else o for o in outs)
+
+
+def fits_fused(n_dp, n_rep, args):
+    tokens, samples = args[0].shape[0], args[2].shape[0]
+    n_dev = n_dp * n_rep
+    rows = [args[i].shape[0] for i in (3, 4, 5)]
+    return (
+        n_dp == 8
+        and n_rep > 1
+        and samples % n_dev == 0
+        and 2 * (samples // n_dev) + 0 <= SUB
+        and samples // n_dev + 2 <= SUB
+        and tokens % samples == 0
+        and (tokens // samples) % 16 == 0
+        and all(r % (16 * n_dp) == 0 for r in rows)
+        and (sum(rows) // n_dp) % (16 * n_rep) == 0
+        and rows[0] == 2 * rows[1]
+    )
+
+
 def solution(mesh):
     in_specs = (
         P(("dp", "rep"), None),
@@ -198,6 +573,13 @@
         P(),
         P(),
     )
-    return jax.shard_map(
-        per_device, mesh=mesh, in_specs=in_specs, out_specs=out_specs, check_vma=False
-    )
+    n_dp, n_rep = mesh.shape["dp"], mesh.shape["rep"]
+
+    def step(*args):
+        fused = fits_fused(n_dp, n_rep, args)
+        body = functools.partial(fused_device, n_dp, n_rep) if fused else per_device
+        return jax.shard_map(
+            body, mesh=mesh, in_specs=in_specs, out_specs=out_specs, check_vma=False
+        )(*args)
+
+    return step

time: 257 us -> 84.4 us (0.33)
  waiting for transfers between devices: 110 us -> 0 us
  blocking collectives: 100 us -> 0 us
  Pallas kernels: 0 us -> 67.2 us
  between operations: 14.1 us -> 0.72 us
  matrix products: 12.8 us -> 0 us
  other arithmetic: 13.6 us -> 3.39 us
  local copies, waits for them, and re-layouts: 5.4 us -> 12.6 us
    reduce_scatter x3 -> x0, waiting for transfers between devices: 109 us -> none  [the longest x1 43.6 us: per_device(): lax.psum_scatter(contract_first(part, normed_b), 'dp', scatter_dimension=...]
    pallas_call x0 -> x1, Pallas kernels: none -> 67.2 us  [fused_device(): pl.pallas_call(functools.partial(fused_kernel, n_rep, n_sam), out_shape=(...]
    all_gather x6 -> x0, blocking collectives: 60.7 us -> none  [the longest x2 20.9 us: fetch(): lax.all_gather(piece_in, 'dp', axis=0, tiled=True)]
    psum x1 -> x0, blocking collectives: 39.6 us -> none  [per_device(): total_gain, total_bias = lax.psum((grad_gain, grad_bias), ('dp', 'rep'))]
    dot_general x11 -> x0, matrix products: 12.8 us -> none  [the longest x3 4.66 us: contract_last(): lax.dot_general(left, right, (((1,), (1,)), ((), ())), preferred_element_...]
    convert_element_type x7 -> x1, other arithmetic: 6.03 us -> 0.08 us  [time_features(): return jax.nn.silu(sinusoid(step_ids, width)).astype(jnp.bfloat16)]
    add x5 -> x0, other arithmetic: 5.73 us -> none  [the longest x4 5.5 us: average(): ema_decay * target_p + (1.0 - ema_decay) * (student_p - learn_rate * grad_p)]
    unnamed x57 -> x38, local copies, waits for them, and re-layouts: 4.17 us -> 9.69 us
  transfers between devices with their start and end apart: 4 -> 0, of which waited for: 4 -> 0; matrix products, arithmetic and copies ran while one was open for 4% -> 0% of each run, Pallas kernels for 0% -> 0%
where the time goes in v1:
time: 84.4 us; the launch traced here: 84 us
  Pallas kernels  67.2 us (80%)
  local copies, waits for them, and re-layouts  12.6 us (15%)
  other arithmetic  3.39 us (4%)
    pallas_call x1, Pallas kernels, fused_device(): pl.pallas_call(functools.partial(fused_kernel, n_rep, n_sam), out_shape=(...  67.2 us
    unnamed x38, local copies, waits for them, and re-layouts  9.69 us
    pallas_call x4, other arithmetic, fused_device(): pl.pallas_call(functools.partial(fused_kernel, n_rep, n_sam), out_shape=(...  2.38 us
    reshape x4, local copies, waits for them, and re-layouts, fused_device(): line = lambda v: v.reshape(1, width)  2.25 us

profile of v1, /device:TPU:0, one launch (start us, length us, event | category | flops | bytes accessed | tf_op | source)
XLA Modules:
  0.0 84.0 jit_solution(3424453068112747694)
XLA Ops:
  0.6 0.0 copy-start.14
  0.7 0.0 copy-start.6
  0.7 0.7 broadcast_add_fusion
  1.4 0.0 copy-done.14
  1.4 0.1 add_convert_fusion
  1.5 0.0 copy-done.6
  1.5 0.0 copy-start.7
  1.5 0.6 reshape.69.sg
  2.0 0.1 copy-done.7
  2.1 0.0 copy-start.8
  2.1 0.6 reshape.70.sb
  2.7 0.1 copy-done.8
  2.8 0.6 reshape.71.tg
  3.4 0.1 copy-done.9
  3.5 0.6 reshape.72.tb
  4.1 0.1 multiply_cosine_fusion
  4.2 0.1 fusion
  4.3 0.1 reshape.77
  4.4 0.6 copy.29
  5.0 0.0 copy-start
  5.0 1.9 %copy.26.x_s = bf16[512,320]{1,0:T(8,128)(2,1)} copy(bf16[512,320]{0,1:T(8,128)(2,1)} %param.13) | data formatting | bytes 655360 | tf_op args[0]
  7.0 0.0 copy-done
  7.0 0.9 %copy.27.x_t = bf16[512,320]{1,0:T(8,128)(2,1)} copy(bf16[512,320]{0,1:T(8,128)(2,1)S(1)} %copy-done) | data formatting | bytes 655360 | tf_op args[1]
  7.9 67.2 %distill_step.1 = (f32[160,320]{1,0:T(8,128)}, f32[80,320]{1,0:T(8,128)}, f32[80,320]{1,0:T(8,128)}, f32[1,320]{1,0:T(1,128)}, f32[1,320]{1,0:T(1,128)}, /*index...) custom-call(bf16[512,320]{1,0:T(8,128)(2,1)} %copy.26.x_s, ...), custom_call_target="tpu_custom_call" | custom-call | tf_op jit(solution)/shard_map/distill_step/pallas_call | solution.py:516
  75.1 0.0 copy-start.13
  75.1 0.7 copy-done.13
  75.8 0.0 copy-start.12
  75.8 0.6 reduce
  76.4 0.1 copy-done.12
  76.5 0.0 copy-start.11
  76.5 0.6 reduce.1
  77.1 0.1 copy-done.11
  77.1 0.0 copy-start.10
  77.1 0.6 reduce.2
  77.7 0.1 copy-done.10
  77.8 0.6 reduce.3
  78.4 0.0 copy-start.5
  78.4 1.7 %copy.36 = f32[160,320]{1,0:T(8,128)} copy(f32[160,320]{1,0:T(8,128)} %get-tuple-element.42) | data formatting | bytes 409600
  80.1 0.0 copy-done.5
  80.1 0.6 copy.37
  80.8 0.0 copy-done.4
  80.8 0.6 copy.38
  81.4 0.0 copy-done.1
  81.4 0.7 copy.39
  82.1 0.3 copy-done.3
  82.4 0.6 copy.40
  83.1 0.3 copy-done.2
  83.3 0.6 copy.41
  (7 shorter events, 0.0 us)
Async XLA Ops:
  0.6 0.7 copy-start.14
  0.7 0.8 copy-start.6
  1.5 0.7 copy-start.7
  2.1 0.7 copy-start.8
  2.8 0.7 copy-start.9
  5.0 1.9 %copy-start = (bf16[512,320]{0,1:T(8,128)(2,1)S(1)}, bf16[512,320]{0,1:T(8,128)(2,1)}, u32[]{:S(2)}) copy-start(bf16[512,320]{0,1:T(8,128)(2,1)} %param.14) | copy-start | bytes 983044
  75.1 0.7 copy-start.13
  75.8 0.7 copy-start.12
  76.5 0.7 copy-start.11
  77.1 0.7 copy-start.10
  78.4 1.7 %copy-start.5 = (f32[80,320]{1,0:T(8,128)S(1)}, f32[80,320]{1,0:T(8,128)}, u32[]{:S(2)}) copy-start(f32[80,320]{1,0:T(8,128)} %get-tuple-element.43) | copy-start | bytes 307204
  78.4 2.4 %copy-start.4 = (f32[80,320]{1,0:T(8,128)S(1)}, f32[80,320]{1,0:T(8,128)}, u32[]{:S(2)}) copy-start(f32[80,320]{1,0:T(8,128)} %get-tuple-element.44) | copy-start | bytes 307204
  80.1 1.3 %copy-start.1 = (f32[160,320]{1,0:T(8,128)S(1)}, f32[160,320]{1,0:T(8,128)}, u32[]{:S(2)}) copy-start(f32[160,320]{1,0:T(8,128)} %get-tuple-element.47) | copy-start | bytes 614404
  81.4 1.0 %copy-start.3 = (f32[80,320]{1,0:T(8,128)S(1)}, f32[80,320]{1,0:T(8,128)}, u32[]{:S(2)}) copy-start(f32[80,320]{1,0:T(8,128)} %get-tuple-element.48) | copy-start | bytes 307204
  82.4 0.9 %copy-start.2 = (f32[80,320]{1,0:T(8,128)S(1)}, f32[80,320]{1,0:T(8,128)}, u32[]{:S(2)}) copy-start(f32[80,320]{1,0:T(8,128)} %get-tuple-element.49) | copy-start | bytes 307204

commit v2 on v1

--- a/solution.py
+++ b/solution.py
@@ -183,7 +183,7 @@
 def fused_kernel(
     n_rep, n_sam,
     x_s, x_t, tf, sw, so, st, sg, sb, tw, to, tt, tg, tb,
-    gw_o, go_o, gt_o, gg_o, gb_o, ew_o, eo_o, et_o, eg_o, eb_o,
+    fin_o, sum_o,
     ws_all, os_all, wt_all, ot_all,
     tf_all, e_part, e_in, small, small_rep,
     normed_v, inv_v, nb_v, hid_v, a_v, b_v, y_v, nbt_v, gyb_v, gma_v, gmb_v,
@@ -196,7 +196,7 @@
     me, rep = lax.axis_index("dp"), lax.axis_index("rep")
     core, col, row = lax.rem(me, 2), lax.rem(lax.div(me, 2), 2), lax.div(me, 4)
     rows_in, rows_out, rows_time = sw.shape[0], so.shape[0], st.shape[0]
-    tokens = x_s.shape[0]
+    tokens, width = x_s.shape[1], x_s.shape[0]
     per = tokens // n_sam
     ff = os_all.shape[0]
 
@@ -295,7 +295,7 @@
         emb = emb + e_in[k]
 
     def normalise(x_ref, k, shift, gain, bias):
-        summed = x_ref[pl.ds(k * per, per), :].astype(f32) + shift
+        summed = x_ref[:, pl.ds(k * per, per)].astype(f32).T + shift
         center = summed - jnp.mean(summed, axis=1, keepdims=True)
         inv = lax.rsqrt(jnp.mean(center * center, axis=1, keepdims=True) + 1e-05)
         normed = center * inv
@@ -303,14 +303,14 @@
 
     for k in range(n_sam):
         at = pl.ds(k * per, per)
-        summed, inv, normed, nb = normalise(x_s, k, emb[k : k + 1], sg[...], sb[...])
+        summed, inv, normed, nb = normalise(x_s, k, emb[k : k + 1], sg[...][None], sb[...][None])
         y_v[at, :], normed_v[at, :], nb_v[at, :] = summed, normed, nb
         inv_v[at, :] = inv
     relay_far(0)
     relay_near(1)
     for k in range(n_sam):
         at = pl.ds(k * per, per)
-        summed, inv, normed, nb = normalise(x_t, k, emb[n_sam + k : n_sam + k + 1], tg[...], tb[...])
+        summed, inv, normed, nb = normalise(x_t, k, emb[n_sam + k : n_sam + k + 1], tg[...][None], tb[...][None])
         y_v[at, :], nbt_v[at, :] = y_v[at, :] - summed, nb
     close_gather(0)
     relay_far(1)
@@ -357,7 +357,7 @@
     for q in range(4):
         to_core(gb_out, r1_out, rows_out, q, q)
 
-    grad_gain = jnp.zeros((1, x_s.shape[1]), f32)
+    grad_gain = jnp.zeros((1, width), f32)
     grad_bias = grad_gain
     embs = []
     for k in range(n_sam):
@@ -371,14 +371,14 @@
         normed = normed_v[at, :]
         grad_gain = grad_gain + jnp.sum(gz * normed, axis=0, keepdims=True)
         grad_bias = grad_bias + jnp.sum(gz, axis=0, keepdims=True)
-        gn = gz * sg[...]
+        gn = gz * sg[...][None]
         gs = y_v[at, :] + inv_v[at, :] * (
             gn
             - jnp.mean(gn, axis=1, keepdims=True)
             - normed * jnp.mean(gn * normed, axis=1, keepdims=True)
         )
         embs.append(jnp.sum(gs, axis=0, keepdims=True))
-    fill = jnp.zeros((SUB - n_sam - 2, x_s.shape[1]), f32)
+    fill = jnp.zeros((SUB - n_sam - 2, width), f32)
     small[pl.ds(me, 1)] = jnp.concatenate(embs + [grad_gain, grad_bias, fill], axis=0)[None]
 
     for h, gm in enumerate((gma_v, gmb_v)):
@@ -413,7 +413,7 @@
     feats = jnp.where(line < n_sam, feats, 0.0)
     p_v[pl.ds(rows_in + rows_out, rows_time), :] = lax.dot_general(
         feats,
-        small[...].reshape(8 * SUB, x_s.shape[1]),
+        small[...].reshape(8 * SUB, width),
         (((0,), (0,)), ((), ())),
         precision=lax.Precision.HIGHEST,
         preferred_element_type=f32,
@@ -444,7 +444,7 @@
     for j in range(1, n_rep):
         arrive(r3_v.at[j], r3_send.at[j], r3_recv.at[j])
         total = total + r3_v[j].astype(f32)
-    fin_v[mine, :] = total
+    fin_v[mine, :] = total.astype(bf16)
     for j in range(1, n_rep):
         part = block(fin_v, rep, share)
         send(part, part, r4_send.at[j], r4_recv.at[j], {"rep": rep_at(j)})
@@ -455,25 +455,34 @@
     for j in range(1, n_rep):
         sums = sums + small_rep[j]
 
-    def average(target_p, student_p, grad_p):
-        return ema_decay * target_p + (1.0 - ema_decay) * (student_p - learn_rate * grad_p)
-
-    gg, gb = sums[n_sam : n_sam + 1], sums[n_sam + 1 : n_sam + 2]
-    gg_o[...], gb_o[...] = gg, gb
-    eg_o[...] = average(tg[...], sg[...], gg)
-    eb_o[...] = average(tb[...], sb[...], gb)
+    sum_o[...] = sums
     for j in range(1, n_rep):
         arrive(block(fin_v, rep_at(n_rep - j), share), r4_send.at[j], r4_recv.at[j])
+    fin_o[...] = fin_v[...]
+    for copy in sends:
+        copy.wait_send()
+
+
+def average(target_p, student_p, grad_p):
+    return ema_decay * target_p + (1.0 - ema_decay) * (student_p - learn_rate * grad_p)
+
+
+def update_kernel(
+    n_sam, fin, sums, sw, so, st, sg, sb, tw, to, tt, tg, tb,
+    gw_o, go_o, gt_o, gg_o, gb_o, ew_o, eo_o, et_o, eg_o, eb_o,
+):
     start = 0
     for g_o, e_o, student, target in (
         (gw_o, ew_o, sw, tw), (go_o, eo_o, so, to), (gt_o, et_o, st, tt),
     ):
-        grad = fin_v[pl.ds(start, g_o.shape[0]), :]
+        grad = fin[pl.ds(start, g_o.shape[0]), :].astype(jnp.float32)
         g_o[...] = grad
         e_o[...] = average(target[...], student[...], grad)
         start += g_o.shape[0]
-    for copy in sends:
-        copy.wait_send()
+    gg, gb = sums[n_sam, :], sums[n_sam + 1, :]
+    gg_o[...], gb_o[...] = gg, gb
+    eg_o[...] = average(tg[...], sg[...], gg)
+    eb_o[...] = average(tb[...], sb[...], gb)
 
 
 def fused_device(n_dp, n_rep, *args):
@@ -505,26 +514,36 @@
         vm((4, rows_in, width), bf16), vm((4, rows_out, width), bf16),
         vm((4, rows_in, width), bf16), vm((4, rows_out, width), bf16),
         vm((rows_all, width), f32), vm((rows_all, width), bf16),
-        vm((n_rep, rows_all // n_rep, width), bf16), vm((rows_all, width), f32),
+        vm((n_rep, rows_all // n_rep, width), bf16), vm((rows_all, width), bf16),
         dma((32,)), dma((32,)), dma((8,)), dma((8,)), dma((8,)), dma((8,)), dma((8,)), dma((8,)),
         dma((8,)), dma((8,)), dma((8,)), dma((8,)),
         dma((n_rep,)), dma((n_rep,)), dma((n_rep,)), dma((n_rep,)), dma((n_rep,)), dma((n_rep,)),
     ]
-    line = lambda v: v.reshape(1, width)
     big = [jax.ShapeDtypeStruct(w.shape, f32) for w in (sw, so, st)]
-    flat = [jax.ShapeDtypeStruct((1, width), f32)] * 2
-    outs = pl.pallas_call(
+    flat = [jax.ShapeDtypeStruct((width,), f32)] * 2
+    fin, sums = pl.pallas_call(
         functools.partial(fused_kernel, n_rep, n_sam),
-        out_shape=(*big, *flat, *big, *flat),
+        out_shape=(
+            jax.ShapeDtypeStruct((rows_all, width), bf16),
+            jax.ShapeDtypeStruct((SUB, width), f32),
+        ),
         in_specs=[pl.BlockSpec(memory_space=vm)] * 13,
-        out_specs=[pl.BlockSpec(memory_space=vm)] * 10,
+        out_specs=[pl.BlockSpec(memory_space=vm)] * 2,
         scratch_shapes=scratch,
         compiler_params=pltpu.CompilerParams(
-            collective_id=0, has_side_effects=True, vmem_limit_bytes=60 * 1024 * 1024
+            collective_id=0, has_side_effects=True, vmem_limit_bytes=56 * 1024 * 1024
         ),
         name="distill_step",
-    )(student_in, target_in, feats, sw, so, st, line(sg), line(sb), tw, to, tt, line(tg), line(tb))
-    return tuple(o.reshape(width) if o.shape[0] == 1 else o for o in outs)
+    )(student_in.T, target_in.T, feats, sw, so, st, sg, sb, tw, to, tt, tg, tb)
+    return tuple(
+        pl.pallas_call(
+            functools.partial(update_kernel, n_sam),
+            out_shape=(*big, *flat, *big, *flat),
+            in_specs=[pl.BlockSpec(memory_space=vm)] * 12,
+            out_specs=[pl.BlockSpec(memory_space=vm)] * 10,
+            name="average_step",
+        )(fin, sums, sw, so, st, sg, sb, tw, to, tt, tg, tb)
+    )
 
 
 def fits_fused(n_dp, n_rep, args):
@@ -538,7 +557,7 @@
         and 2 * (samples // n_dev) + 0 <= SUB
         and samples // n_dev + 2 <= SUB
         and tokens % samples == 0
-        and (tokens // samples) % 16 == 0
+        and (tokens // samples) % 128 == 0
         and all(r % (16 * n_dp) == 0 for r in rows)
         and (sum(rows) // n_dp) % (16 * n_rep) == 0
         and rows[0] == 2 * rows[1]

time: 84.4 us -> 67.1 us (0.80)
  local copies, waits for them, and re-layouts: 12.6 us -> 1.35 us
  other arithmetic: 3.39 us -> 0.31 us
  Pallas kernels: 67.2 us -> 64.5 us
    unnamed x38 -> x2, local copies, waits for them, and re-layouts: 9.69 us -> 0.65 us
    pallas_call x1, Pallas kernels: 67.2 us -> 62.1 us  [fused_device(): pl.pallas_call(functools.partial(fused_kernel, n_rep, n_sam), out_shape=(...]
    pallas_call x0 -> x1, Pallas kernels: none -> 2.49 us  [fused_device(): pl.pallas_call(functools.partial(update_kernel, n_sam), out_shape=(*big,...]
    pallas_call x4 -> x0, other arithmetic: 2.38 us -> none  [fused_device(): pl.pallas_call(functools.partial(fused_kernel, n_rep, n_sam), out_shape=(...]
    reshape x4 -> x0, local copies, waits for them, and re-layouts: 2.25 us -> none  [fused_device(): line = lambda v: v.reshape(1, width)]
where the time goes in v2:
time: 67.1 us; the launch traced here: 66.9 us
  Pallas kernels  64.5 us (96%)
  local copies, waits for them, and re-layouts  1.35 us (2%)
  between operations  0.68 us (1%)
    pallas_call x1, Pallas kernels, fused_device(): pl.pallas_call(functools.partial(fused_kernel, n_rep, n_sam), out_shape=(...  62.1 us
    pallas_call x1, Pallas kernels, fused_device(): pl.pallas_call(functools.partial(update_kernel, n_sam), out_shape=(*big,...  2.49 us

profile of v2, /device:TPU:0, one launch (start us, length us, event | category | flops | bytes accessed | tf_op | source)
XLA Modules:
  0.0 66.9 jit_solution(5037956324792638618)
XLA Ops:
  0.6 0.0 copy-start
  0.7 0.6 copy-done
  1.3 0.1 add_convert_fusion
  1.4 0.1 multiply_cosine_fusion
  1.5 0.1 fusion
  1.6 0.1 reshape.45
  1.7 0.6 copy.25
  2.3 62.1 %distill_step.1 = (bf16[320,320]{1,0:T(8,128)(2,1)}, f32[8,320]{1,0:T(8,128)}) custom-call(bf16[320,512]{1,0:T(8,128)(2,1)} %bitcast.5, bf16[320,512]{1,0:T(8,128)(2,1)} %bitcast.6, f32[8,8,80]{2,1,0:T(8,128)} %bitcast.7, f32[160,320]{1,0:T(8,128)} %sw.3, f32[80,320]{1,0:T(8,128)} %so.3, f32[80,320]{1,0:T(8,128)} %st.3, f32[320]{0:T(512)} %sg.3, f32[320]{0:T(512)} %sb.3, ...), custom_call_target="tpu_custom_call" | custom-call | tf_op jit(solution)/shard_map/distill_step/pallas_call | solution.py:524
  64.4 2.5 %average_step.1 = (f32[160,320]{1,0:T(8,128)}, f32[80,320]{1,0:T(8,128)}, f32[80,320]{1,0:T(8,128)}, f32[320]{0:T(512)}, f32[320]{0:T(512)}, /*index=5*/f32[160,...) custom-call(bf16[320,320]{1,0:T(8,128)(2,1)} %get-tuple-element.12.fin, ...), custom_call_target="tpu_custom_call" | custom-call | tf_op jit(solution)/shard_map/average_step/pallas_call | solution.py:539
  (3 shorter events, 0.0 us)
Async XLA Ops:
  0.6 0.7 copy-start
